TPU v7x, 512 devices: a whole 4x4x16 slice. The times are simulated.
512 devices in a mesh: pole: 8 (over z_lo), grid: 64 (over x, z_hi, y, core).
Axes of the slice: x: 4, y: 4, z: 16 (z_hi: 2, z_lo: 8; z = z_hi * 8 + z_lo), core: 2. Of those that a mesh axis runs over, the one named last changes fastest.
Arguments:
- inverse_rows: bfloat16 [8, 2, 8192, 8192], P('pole', None, 'grid'), may hold values from -0.09375 to 0.09375
- factor: bfloat16 [8, 2, 2048, 2, 512], P('pole', None, 'grid'), may hold values from -0.8984375 to 0.8984375
- diag_inverse: float32 [8, 2, 512, 2, 512], P('pole', None, None, None, 'grid'), may hold values from -6 to 6
- pole_weights: float32 [8, 2], P('pole'), may hold values from -3 to 3
- structure: int32 [2, 4], replicated, may hold values from 0 to 15, as said below
- row_owner: int32 [16], replicated, may hold values from 0 to 15, each once
Outputs:
- column_sum: float32 [2, 8192, 2, 512], P(None, 'grid', None, 'pole')
- diagonal_sum: float32 [2, 512, 2, 512], P(None, 'pole', None, 'grid')
Inputs may be any that keep to these rules, and one draw needn't show every extreme that they name: `structure`: row k lists 4 distinct ancestors of supernode k in ascending order. A permutation: ancestor a's block row is stored as block row row_owner[a].
All inputs are finite; a program needn't handle non-finite values.
Results may differ from a plain program's by a relative error of at most 0.0029.
Values may be sent and summed in bfloat16 or wider, within the bound.
A program may use at most 64 MiB of HBM per device.

v0:
```python
import jax
import jax.numpy as jnp
from jax import lax
from jax.sharding import PartitionSpec as P

BLOCK = 512
ANCESTORS = 16
LISTED = 4
SNODES = 2


def side_by_side(arrays, axis, dim, along):
    ends, at = ([], 0)
    for a in arrays[:-1]:
        at += a.shape[along]
        ends.append(at)
    both = jnp.concatenate(arrays, axis=along)
    return tuple(jnp.split(lax.all_gather(both, axis, axis=dim, tiled=True), ends, axis=along))


def copy_for_each(array, axis):
    devices = lax.axis_size(axis)
    return lax.all_to_all(
        jnp.broadcast_to(array[None], (devices, *array.shape)), axis, 0, 0, tiled=True
    )


def joined_along(blocks, dim):
    dims = list(blocks.shape[1:])
    dims[dim] *= blocks.shape[0]
    return jnp.moveaxis(blocks, 0, dim).reshape(dims)


def gather_directly(array, axis, dim):
    blocks = copy_for_each(array, axis)
    return joined_along(blocks, dim)


def cut_along(array, dim, devices):
    before, after = (array.shape[:dim], array.shape[dim + 1 :])
    return jnp.moveaxis(array.reshape(*before, devices, -1, *after), dim, 0)


def sum_at_owner(array, axis, dim):
    devices = lax.axis_size(axis)
    blocks = lax.all_to_all(cut_along(array, dim, devices), axis, 0, 0, tiled=True)
    return jnp.sum(blocks, axis=0)


def complex_scale(weight_pair, values):
    real_part = values[..., 0, :]
    imag_part = values[..., 1, :]
    return jnp.stack(
        [
            weight_pair[0] * real_part - weight_pair[1] * imag_part,
            weight_pair[0] * imag_part + weight_pair[1] * real_part,
        ],
        axis=-2,
    )


def accumulate(chosen, block_rows):
    height = block_rows.shape[0]
    running = jnp.dot(
        chosen, block_rows.reshape(height, 2 * BLOCK), preferred_element_type=jnp.float32
    )
    return (running, block_rows)


def body(inverse_rows, factor, diag_inverse, pole_weights, structure, row_owner):
    rows_dev = inverse_rows.shape[2]
    grid_count = lax.axis_size("grid")
    grid_id = lax.axis_index("grid")
    slot_held = grid_id * rows_dev // BLOCK
    ancestor_ids = jnp.arange(ANCESTORS, dtype=jnp.int32)
    ancestor_held = jnp.sum(jnp.where(row_owner == slot_held, ancestor_ids, 0))
    local_rows = inverse_rows[0]
    span_rows = LISTED * BLOCK
    selections = []
    for snode_id in range(SNODES):
        listed = structure[snode_id]
        active = jnp.any(listed == ancestor_held).astype(jnp.bfloat16)
        pieces = [
            lax.dynamic_slice_in_dim(local_rows, listed[position] * BLOCK, BLOCK, 2)
            for position in range(LISTED)
        ]
        chosen = jnp.concatenate(pieces, axis=2).reshape(2 * rows_dev, span_rows) * active
        selections.append(chosen)
    sums = []
    factors = []
    block_rows = side_by_side((factor[0, 0], factor[0, 1]), "grid", 0, 1)
    first_pair = accumulate(selections[0], block_rows[0])
    second_pair = accumulate(selections[1], block_rows[1])
    sums = [first_pair[0], second_pair[0]]
    factors = [first_pair[1], second_pair[1]]
    columns = []
    for snode_id in range(SNODES):
        product = sums[snode_id]
        real_part = product[rows_dev:, BLOCK:] - product[:rows_dev, :BLOCK]
        imag_part = -(product[:rows_dev, BLOCK:] + product[rows_dev:, :BLOCK])
        columns.append(jnp.stack([real_part, imag_part], axis=1))
    column_rounded = jnp.stack(columns).astype(jnp.bfloat16)
    col_share = BLOCK // grid_count
    sendable = column_rounded.reshape(SNODES, rows_dev, 2, grid_count, col_share)
    received = lax.all_to_all(sendable, "grid", split_axis=3, concat_axis=1, tiled=True)
    width_now = received.shape[4]
    outputs = []
    for snode_id in range(SNODES):
        listed = structure[snode_id]
        gathered_rows = jnp.concatenate(
            [
                lax.dynamic_slice_in_dim(
                    received[snode_id], row_owner[listed[position]] * BLOCK, BLOCK, 0
                )
                for position in range(LISTED)
            ],
            axis=0,
        )
        right_part = gathered_rows.reshape(span_rows, 2 * width_now)
        moment = lax.dot_general(
            factors[snode_id].reshape(span_rows, 2 * BLOCK),
            right_part,
            (((0,), (0,)), ((), ())),
            preferred_element_type=jnp.float32,
        )
        diag_real = moment[:BLOCK, :width_now] - moment[BLOCK:, width_now:]
        diag_imag = moment[:BLOCK, width_now:] + moment[BLOCK:, :width_now]
        outputs.append(-jnp.stack([diag_real, diag_imag], axis=1)[:, :, None, :])
    diag_terms = jnp.stack(outputs)
    diag_pole = diag_inverse[0] + diag_terms.reshape(SNODES, BLOCK, 2, col_share)
    weight_pair = pole_weights[0]
    pole_count = lax.axis_size("pole")
    pole_share = BLOCK // pole_count
    outgoing = column_rounded.reshape(SNODES, rows_dev, 2, pole_count, pole_share)
    incoming = lax.all_to_all(outgoing, "pole", split_axis=3, concat_axis=3, tiled=True)
    weights_all = gather_directly(pole_weights, "pole", 0)
    real_in = incoming[:, :, 0].astype(jnp.float32)
    imag_in = incoming[:, :, 1].astype(jnp.float32)
    weight_real = weights_all[:, 0][None, None, :, None]
    weight_imag = weights_all[:, 1][None, None, :, None]
    sum_real = jnp.sum(weight_real * real_in - weight_imag * imag_in, axis=2)
    sum_imag = jnp.sum(weight_real * imag_in + weight_imag * real_in, axis=2)
    column_sum = jnp.stack([sum_real, sum_imag], axis=2)
    diagonal_sum = sum_at_owner(complex_scale(weight_pair, diag_pole), "pole", 1)
    return (column_sum, diagonal_sum)


def solution(mesh):
    in_specs = (
        P("pole", None, "grid", None),
        P("pole", None, "grid", None, None),
        P("pole", None, None, None, "grid"),
        P("pole", None),
        P(),
        P(),
    )
    out_specs = (P(None, "grid", None, "pole"), P(None, "pole", None, "grid"))
    return jax.shard_map(body, mesh=mesh, in_specs=in_specs, out_specs=out_specs, check_vma=False)
```

profile of v0, /device:TPU:1, one launch (start us, length us, event | category | flops | bytes accessed | tf_op | source)
XLA Modules:
  0.0 308.5 jit_solution(1616198991086849570)
XLA Ops:
  7.2 0.0 all-gather.2.cloned.1.call-start
  7.2 1.0 slice_bitcast_fusion.3
  8.2 0.8 pad_maximum_fusion
  9.0 0.0 all-gather.2.cloned.1.call-update
  9.0 1.3 broadcast_in_dim.15
  10.2 13.1 %all-to-all-start = ((f32[8,1,2]{2,1,0:T(1,128)}), f32[8,1,2]{2,1,0:T(1,128)S(1)}, u32[]{:S(2)}, u32[]{:S(2)}) async-start(f32[8,1,2]{2,1,0:T(1,128)} %broadcast_in_dim.15), calls=%async_computation | async-start | bytes 8192 | tf_op jit(solution)/shard_map/all_to_all | solution.py:23
  23.3 1.6 fusion.52
  30.1 1.3 fusion.45
  31.4 2.0 compare_reduce_fusion.1
  34.6 1.8 constant_dynamic-slice_fusion.15
  36.4 147.4 %all-gather.2.cloned.1.call-done = bf16[2048,4,512]{2,1,0:T(4,128)(2,1)} async-done(((bf16[32,4,512]{2,1,0:T(4,128)(2,1)}), bf16[2048,4,512]{2,1,0:T(4,128)(2,1)}) %all-gather.2.cloned.1.call-update) | async-done | bytes 8388624 | tf_op jit(solution)/shard_map/all_gather | solution.py:18
  183.8 10.8 %fusion.50 = (bf16[2048,2,512]{2,1,0:T(2,128)(2,1)}, bf16[2048,2,512]{2,1,0:T(2,128)(2,1)S(1)}) fusion(bf16[2048,4,512]{2,1,0:T(4,128)(2,1)} %all-gather.2.cloned.1.call-done), kind=kLoop, calls=%fused_computation.101 | loop fusion | bytes 16777216 | tf_op jit(solution)/shard_map/split | solution.py:18
  194.6 1.2 copy.39
  195.8 0.0 copy-start
  195.8 1.3 fusion.7
  197.1 0.6 copy-done
  197.7 0.1 fusion.22
  197.8 0.1 copy.22
  197.9 0.1 copy.21
  198.1 3.4 %copy.38 = bf16[256,8,2,512]{3,1,2,0:T(8,128)(2,1)S(1)} copy(bf16[256,8,2,512]{3,2,1,0:T(2,128)(2,1)} %bitcast.121) | data formatting | bytes 8388608
  201.5 0.0 copy-start.2
  201.5 1.3 fusion
  202.8 0.7 copy-done.2
  203.4 0.0 copy-start.4
  203.4 0.0 copy-start.5
  203.4 0.1 fusion.25
  203.5 0.1 copy.20
  203.7 0.1 copy.19
  203.8 0.1 maximum_maximum_fusion.1
  203.8 0.9 copy.29
  204.8 0.0 all-to-all-done
  204.8 5.9 %all-to-all-start.2 = ((bf16[2,128,2,64,8]{1,4,2,0,3:T(8,128)(2,1)}), bf16[2,128,2,64,8]{1,4,2,0,3:T(8,128)(2,1)S(1)}, u32[]{:S(2)}, u32[]{:S(2)}) async-start(bf16[2,128,2,64,8]{1,4,2,0,3:T(8,128)(2,1)} %copy.29), calls=%async_computation.2 | async-start | bytes 1048576 | tf_op jit(solution)/shard_map/all_to_all | solution.py:105
  226.0 0.0 copy-done.4
  226.1 0.7 fusion.54
  231.8 0.0 copy-done.5
  231.8 0.6 fusion.53
  232.3 0.1 copy.18
  232.5 0.9 copy.23
  233.4 10.7 %all-to-all-done.2 = bf16[2,128,2,64,8]{1,4,2,0,3:T(8,128)(2,1)S(1)} async-done(((bf16[2,128,2,64,8]{1,4,2,0,3:T(8,128)(2,1)}), bf16[2,128,2,64,8]{1,4,2,0,3:T(8,128)(2,1)S(1)}, u32[]{:S(2)}, u32[]{:S(2)}) %all-to-all-start.2) | async-done | bytes 524320 | tf_op jit(solution)/shard_map/all_to_all | solution.py:105
  244.1 13.0 %all-to-all-start.1 = ((bf16[2,128,2,8,64]{1,4,2,0,3:T(8,128)(2,1)}), bf16[2,128,2,8,64]{1,4,2,0,3:T(8,128)(2,1)S(1)}, u32[]{:S(2)}, u32[]{:S(2)}) async-start(bf16[2,128,2,8,64]{1,4,2,0,3:T(8,128)(2,1)} %copy.23), calls=%async_computation.1 | async-start | bytes 1048576 | tf_op jit(solution)/shard_map/all_to_all | solution.py:135
  257.1 0.1 copy.30
  257.2 0.1 squeeze.42
  257.3 0.1 copy.31
  257.4 0.1 squeeze.43
  257.5 0.0 copy-start.1
  257.6 0.0 copy-start.3
  257.6 3.0 fusion.26
  260.6 0.4 copy-done.1
  261.0 0.7 fusion.33
  261.6 0.0 copy-done.3
  261.7 1.3 multiply_subtract_fusion
  263.0 0.1 stack.103
  263.1 0.1 stack.102
  263.2 0.7 reshape.220
  263.9 14.2 %all-to-all-done.1 = bf16[2,128,2,8,64]{1,4,2,0,3:T(8,128)(2,1)S(1)} async-done(((bf16[2,128,2,8,64]{1,4,2,0,3:T(8,128)(2,1)}), bf16[2,128,2,8,64]{1,4,2,0,3:T(8,128)(2,1)S(1)}, u32[]{:S(2)}, u32[]{:S(2)}) %all-to-all-start.1) | async-done | bytes 524320 | tf_op jit(solution)/shard_map/all_to_all | solution.py:135
  278.1 11.7 %all-to-all-start.3 = ((f32[8,1,2048]{2,1,0:T(1,128)}), f32[8,1,2048]{2,1,0:T(1,128)S(1)}, u32[]{:S(2)}, u32[]{:S(2)}) async-start(f32[8,1,2048]{2,1,0:T(1,128)} %reshape.220), calls=%async_computation.3 | async-start | bytes 131072 | tf_op jit(solution)/shard_map/all_to_all | solution.py:46
  289.9 0.3 fusion.15
  290.1 0.7 pad_maximum_fusion.1
  290.8 8.8 %all-to-all-done.3 = f32[8,1,2048]{2,1,0:T(1,128)S(1)} async-done(((f32[8,1,2048]{2,1,0:T(1,128)}), f32[8,1,2048]{2,1,0:T(1,128)S(1)}, u32[]{:S(2)}, u32[]{:S(2)}) %all-to-all-start.3) | async-done | bytes 65568 | tf_op jit(solution)/shard_map/all_to_all | solution.py:46
  299.6 0.5 broadcast.9
  300.2 0.8 reduce.2
  301.0 0.1 reshape.221
  301.1 0.6 copy.35
  (13 shorter events, 0.2 us)
Async XLA Ops:
  7.2 176.6 %all-gather.2.cloned.1.call-start = ((), (), s32[]{:S(2)}) async-start(), calls=%async_computation.4 | async-start | bytes 8519680 | tf_op jit(solution)/shard_map/all_gather | solution.py:18
  10.2 194.5 %all-to-all-start = ((f32[8,1,2]{2,1,0:T(1,128)}), f32[8,1,2]{2,1,0:T(1,128)S(1)}, u32[]{:S(2)}, u32[]{:S(2)}) async-start(f32[8,1,2]{2,1,0:T(1,128)} %broadcast_in_dim.15), calls=%async_computation | async-start | bytes 8192 | tf_op jit(solution)/shard_map/all_to_all | solution.py:23
  195.8 1.9 copy-start
  201.5 2.0 copy-start.2
  203.4 22.6 %copy-start.4 = (s32[16]{0:T(128)S(1)}, s32[16]{0:T(128)}, u32[]{:S(2)}) copy-start(s32[16]{0:T(128)} %param.11) | copy-start | bytes 196
  203.4 28.3 %copy-start.5 = (f32[1,2]{1,0:T(1,128)S(1)}, f32[1,2]{1,0:T(1,128)}, u32[]{:S(2)}) copy-start(f32[1,2]{1,0:T(1,128)} %param.9) | copy-start | bytes 28
  204.8 39.3 %all-to-all-start.2 = ((bf16[2,128,2,64,8]{1,4,2,0,3:T(8,128)(2,1)}), bf16[2,128,2,64,8]{1,4,2,0,3:T(8,128)(2,1)S(1)}, u32[]{:S(2)}, u32[]{:S(2)}) async-start(bf16[2,128,2,64,8]{1,4,2,0,3:T(8,128)(2,1)} %copy.29), calls=%async_computation.2 | async-start | bytes 1048576 | tf_op jit(solution)/shard_map/all_to_all | solution.py:105
  244.1 34.1 %all-to-all-start.1 = ((bf16[2,128,2,8,64]{1,4,2,0,3:T(8,128)(2,1)}), bf16[2,128,2,8,64]{1,4,2,0,3:T(8,128)(2,1)S(1)}, u32[]{:S(2)}, u32[]{:S(2)}) async-start(bf16[2,128,2,8,64]{1,4,2,0,3:T(8,128)(2,1)} %copy.23), calls=%async_computation.1 | async-start | bytes 1048576 | tf_op jit(solution)/shard_map/all_to_all | solution.py:135
  257.5 3.5 %copy-start.1 = (bf16[256,8,2,512]{3,1,2,0:T(8,128)(2,1)S(1)}, bf16[256,8,2,512]{3,1,2,0:T(8,128)(2,1)}, u32[]{:S(2)}) copy-start(bf16[256,8,2,512]{3,1,2,0:T(8,128)(2,1)} %copy-done) | copy-start | bytes 12582916
  257.6 4.1 %copy-start.3 = (f32[1,2,512,2,8]{2,4,3,1,0:T(8,128)S(1)}, f32[1,2,512,2,8]{2,4,3,1,0:T(8,128)}, u32[]{:S(2)}) copy-start(f32[1,2,512,2,8]{2,4,3,1,0:T(8,128)} %param.8) | copy-start | bytes 196612
  278.1 21.5 %all-to-all-start.3 = ((f32[8,1,2048]{2,1,0:T(1,128)}), f32[8,1,2048]{2,1,0:T(1,128)S(1)}, u32[]{:S(2)}, u32[]{:S(2)}) async-start(f32[8,1,2048]{2,1,0:T(1,128)} %reshape.220), calls=%async_computation.3 | async-start | bytes 131072 | tf_op jit(solution)/shard_map/all_to_all | solution.py:46
Sparse Core Ops, SparseCore 0:
  13.0 170.7 all-gather.1
where the time goes:
time: 310 us; the launch traced here: 309 us
  waiting for transfers between devices  181 us (58%)
  starting transfers between devices  43.8 us (14%)
  between operations  41 us (13%)
  local copies, waits for them, and re-layouts  28.8 us (9%)
  other arithmetic  7.44 us (2%)
  matrix products  6.24 us (2%)
    all_gather x1, waiting for transfers between devices, side_by_side(): lax.all_gather(both, axis, axis=dim, tiled=True)  147 us
    all_to_all x1, waiting for transfers between devices, body(): lax.all_to_all(outgoing, 'pole', split_axis=3, concat_axis=3, tiled=True)  14.2 us
    all_to_all x1, starting transfers between devices, copy_for_each(): lax.all_to_all(jnp.broadcast_to(array[None], (devices, *array.shape)), ax...  13.1 us
    all_to_all x1, starting transfers between devices, body(): lax.all_to_all(outgoing, 'pole', split_axis=3, concat_axis=3, tiled=True)  13 us
    all_to_all x1, starting transfers between devices, sum_at_owner(): lax.all_to_all(cut_along(array, dim, devices), axis, 0, 0, tiled=True)  11.7 us
    split x1, local copies, waits for them, and re-layouts, side_by_side(): jnp.split(lax.all_gather(both, axis, axis=dim, tiled=True), ends, axis=al...  10.8 us
    all_to_all x1, waiting for transfers between devices, body(): lax.all_to_all(sendable, 'grid', split_axis=3, concat_axis=1, tiled=True)  10.7 us
    all_to_all x1, waiting for transfers between devices, sum_at_owner(): lax.all_to_all(cut_along(array, dim, devices), axis, 0, 0, tiled=True)  8.84 us
  transfers between devices with their start and end apart: 5, of which 4 were waited for; matrix products, arithmetic and copies ran while one was open for 12% of the time, Pallas kernels for 0%

commit v1 on v0

v1 whole, which is shorter than its diff:
```python
import jax
import jax.numpy as jnp
from jax import lax
from jax.experimental import pallas as pl
from jax.experimental.pallas import tpu as pltpu
from jax.sharding import PartitionSpec as P

BLOCK = 512
LISTED = 4
SNODES = 2
POLES = 8
PLANES = 2
SIDE = 4
IN_PLANE = 32
RING = 16
LANES = 128
ROWS = 128
SHARD = 32
MESH = pl.DeviceIdType.MESH
DOT = (((1,), (0,)), ((), ()))

ORDER = (
    (0, 0), (1, 0), (0, 2), (2, 0), (1, 2), (3, 0), (2, 2), (0, 1), (4, 0), (3, 2), (1, 1), (4, 2),
    (0, 3), (2, 1), (1, 3), (3, 1), (2, 3), (4, 1), "first", (3, 3), (4, 3), "second",
)
ROUNDS = ((0, 0), (0, 1), (1, 0), (1, 1))


def kernel(
    structure, row_owner, weights, factor, rows_hbm, diag,
    column_out, diag_out,
    fbuf, rows, esend, erecv, tsend, trecv, dsend, drecv, wrows,
    rows_sem, ag_sem, cross_sem, pair_sem, erecv_sem, trecv_sem, drecv_sem, wrecv_sem,
    ag_sent, cross_sent, esent, tsent, dsent, wsent,
):
    pole = lax.axis_index("pole")
    grid = lax.axis_index("grid")
    x, plane = grid // 16, (grid // 8) % 2
    y, core = (grid // 2) % 4, grid % 2
    seat = x * 8 + y * 2 + core
    height = plane * 8 + pole

    def at(x_to, plane_to, y_to, core_to):
        return x_to * 16 + plane_to * 8 + y_to * 2 + core_to

    def along(first, second, core_to=core, plane_to=plane):
        x_to = (x + core * first + (1 - core) * second) % SIDE
        y_to = (y + (1 - core) * first + core * second) % SIDE
        return at(x_to, plane_to, y_to, core_to)

    def seat_grid(seat_to):
        return at(seat_to // 8, plane, (seat_to // 2) % 4, seat_to % 2)

    def height_device(height_to):
        return (height_to % 8, at(x, height_to // 8, y, core))

    load_rows = pltpu.make_async_copy(rows_hbm, rows, rows_sem)
    load_rows.start()

    part = lax.broadcasted_iota(jnp.int32, (8, LANES), 0)
    wrows[pole] = jnp.where(part == 0, weights[0, 0], weights[0, 1])

    barrier = pltpu.get_barrier_semaphore()

    def greet_seat(step, carry):
        target = seat_grid((seat + step) % IN_PLANE)
        pl.semaphore_signal(barrier, inc=1, device_id=(pole, target), device_id_type=MESH)
        return carry

    def greet_height(step, carry):
        target = height_device((height + step) % RING)
        pl.semaphore_signal(barrier, inc=1, device_id=target, device_id_type=MESH)
        return carry

    lax.fori_loop(1, IN_PLANE, greet_seat, 0)
    lax.fori_loop(1, RING, greet_height, 0)
    for k in range(SNODES):
        fbuf[k, grid] = factor[k]
    pl.semaphore_wait(barrier, IN_PLANE - 1 + RING - 1)

    def copy(src, dst, sent, received, device):
        return pltpu.make_async_remote_copy(
            src_ref=src, dst_ref=dst, send_sem=sent, recv_sem=received,
            device_id=device, device_id_type=MESH,
        )

    def cross(k):
        return copy(
            factor.at[k], fbuf.at[k, grid], cross_sent.at[k], cross_sem.at[k],
            height_device((height + 8) % RING),
        )

    for k in range(SNODES):
        cross(k).start()

    def wait_for(ref, sem):
        pltpu.make_async_copy(ref, ref, sem).wait()

    def push(r, src, slot, offset, sem_index):
        k = ROUNDS[r][0]
        first, second = offset
        copy(
            src, slot, ag_sent.at[k], ag_sem.at[r, sem_index],
            (pole, along(first, second)),
        ).start()

    def stage(step, r):
        k, other = ROUNDS[r]
        source_plane = plane if other == 0 else 1 - plane

        def shard(first, second):
            return fbuf.at[k, along(first, second, plane_to=source_plane)]

        def half(ref, which):
            return ref.at[pl.ds(16 * which, 16)]

        own = factor.at[k] if other == 0 else shard(0, 0)

        def to_sibling(src, first, second):
            copy(
                src, shard(first, second), ag_sent.at[k], pair_sem.at[k],
                (pole, at(x, plane, y, 1 - core)),
            ).start()

        def start_second(src, first, index):
            slot = shard(first, 0)
            push(r, src, slot, (0, 1), 4 + 4 * index)
            push(r, src, slot, (0, -1), 5 + 4 * index)

        def turn_second(first, index):
            base = 4 + 4 * index
            low = shard(first, -1)
            wait_for(low, ag_sem.at[r, base])
            push(r, half(low, 0), half(low, 0), (0, 1), base + 2)
            to_sibling(low, first, -1)
            high = shard(first, 1)
            wait_for(high, ag_sem.at[r, base + 1])
            push(r, half(high, 1), half(high, 1), (0, -1), base + 3)
            to_sibling(high, first, 1)

        def end_second(first, index):
            base = 4 + 4 * index
            far = shard(first, 2)
            wait_for(half(far, 0), ag_sem.at[r, base + 2])
            wait_for(half(far, 1), ag_sem.at[r, base + 3])
            to_sibling(far, first, 2)

        if step == 0:
            if other == 1:
                cross(k).wait_recv()
            push(r, own, shard(0, 0), (1, 0), 0)
            push(r, own, shard(0, 0), (-1, 0), 1)
            start_second(own, 0, 0)
            to_sibling(own, 0, 0)
        if step == 1:
            low = shard(-1, 0)
            wait_for(low, ag_sem.at[r, 0])
            push(r, half(low, 0), half(low, 0), (1, 0), 2)
            start_second(low, -1, 1)
            to_sibling(low, -1, 0)
            high = shard(1, 0)
            wait_for(high, ag_sem.at[r, 1])
            push(r, half(high, 1), half(high, 1), (-1, 0), 3)
            start_second(high, 1, 2)
            to_sibling(high, 1, 0)
            turn_second(0, 0)
        if step == 2:
            far = shard(2, 0)
            wait_for(half(far, 0), ag_sem.at[r, 2])
            wait_for(half(far, 1), ag_sem.at[r, 3])
            start_second(far, 2, 3)
            to_sibling(far, 2, 0)
            turn_second(-1, 1)
            turn_second(1, 2)
            end_second(0, 0)
        if step == 3:
            turn_second(2, 3)
            end_second(-1, 1)
            end_second(1, 2)
        if step == 4:
            end_second(2, 3)

    lane = lax.broadcasted_iota(jnp.int32, (1, LANES), 1)
    sign = jnp.where(lane < 64, -1.0, 1.0).astype(jnp.float32)

    def turned(values):
        return sign * pltpu.roll(values, 64, 1)

    def weight_send(step):
        return copy(
            wrows.at[pole], wrows.at[pole], wsent, wrecv_sem,
            ((pole + step) % POLES, grid),
        )

    def columns(k):
        wait_for(fbuf.at[k, pl.ds(0, IN_PLANE)], pair_sem.at[k])
        active = 0
        for i in range(LISTED):
            active = active + jnp.where(owners[k][i] == grid // 4, 1, 0)
        active = active.astype(jnp.float32)
        for n in range(4):
            product = jnp.zeros((2 * ROWS, 2 * LANES), jnp.float32)
            for i in range(LISTED):
                start = structure[k, i] * BLOCK
                block = fbuf[k, pl.ds(16 * i, 16), :, pl.ds(256 * n, 256)].reshape(BLOCK, 256)
                product = product + lax.dot_general(
                    rows[:, pl.ds(start, BLOCK)], block, DOT, preferred_element_type=jnp.float32
                )
            flipped = []
            for u in range(2):
                lanes = slice(LANES * u, LANES * (u + 1))
                value = -(product[:ROWS, lanes] + turned(product[ROWS:, lanes]))
                rounded = (value * active).astype(jnp.bfloat16)
                esend[k, 2 * n + u] = rounded
                flipped.append(jnp.transpose(rounded.astype(jnp.float32)))
            for h in range(8):
                pieces = [
                    flipped[u][64 * part_id + 8 * h : 64 * part_id + 8 * h + 8]
                    for part_id in range(2)
                    for u in range(2)
                ]
                tsend[k, 8 * n + h] = jnp.concatenate(pieces, axis=0).astype(jnp.bfloat16)

        def send_column(step, carry):
            target = (pole + step) % POLES
            copy(
                esend.at[k, target], erecv.at[k, pole], esent.at[k], erecv_sem.at[k],
                (target, grid),
            ).start()
            return carry

        def send_tile(step, carry):
            target = (seat + step) % IN_PLANE
            copy(
                tsend.at[k, target], trecv.at[k, seat], tsent.at[k], trecv_sem.at[k],
                (pole, seat_grid(target)),
            ).start()
            return carry

        lax.fori_loop(1, IN_PLANE, send_tile, 0)
        lax.fori_loop(1, POLES, send_column, 0)
        erecv[k, pole] = esend[k, pole]
        trecv[k, seat] = tsend[k, seat]

    def moments(k):
        wait_for(trecv.at[k, pl.ds(0, IN_PLANE - 1)], trecv_sem.at[k])
        total = jnp.zeros((SHARD, 2 * BLOCK), jnp.float32)
        for i in range(LISTED):
            left = jnp.zeros((SHARD, BLOCK), jnp.bfloat16)
            for slot in range(8):
                place = (slot // 2) * 4 + plane * 2 + slot % 2
                here = jnp.where(owners[k][i] == place, 1.0, 0.0).astype(jnp.bfloat16)
                tiles = [trecv[k, 4 * slot + q] for q in range(4)]
                left = left + here * jnp.concatenate(tiles, axis=1)
            block = fbuf[k, pl.ds(16 * i, 16)].reshape(BLOCK, 2 * BLOCK)
            total = total + lax.dot_general(left, block, DOT, preferred_element_type=jnp.float32)
        weight_real, weight_imag = weights[0, 0], weights[0, 1]
        for j in range(POLES):
            lanes = slice(LANES * j, LANES * (j + 1))
            moment = total[:16, lanes] + turned(total[16:, lanes])
            for side in range(2):
                mine = jnp.where(plane == side, 1.0, 0.0).astype(jnp.float32)
                value = mine * diag[k, :, lanes] - moment[8 * side : 8 * side + 8]
                dsend[8 * side + j, k] = weight_real * value + weight_imag * turned(value)

    owners = []
    for k in range(SNODES):
        owners.append([])
        for i in range(LISTED):
            owner = 0
            for ancestor in range(16):
                owner = owner + jnp.where(structure[k, i] == ancestor, row_owner[ancestor], 0)
            owners[k].append(owner)

    for step in range(1, POLES):
        weight_send(step).start()

    for entry in ORDER:
        if entry == "first":
            load_rows.wait()
            columns(0)
        elif entry == "second":
            columns(1)
        else:
            stage(*entry)

    for k in range(SNODES):
        moments(k)

    def send_diag(step, carry):
        target = (height + step) % RING
        copy(
            dsend.at[target], drecv.at[height], dsent, drecv_sem, height_device(target)
        ).start()
        return carry

    lax.fori_loop(1, RING, send_diag, 0)
    drecv[height] = dsend[height]

    wait_for(wrows.at[pl.ds(0, POLES - 1)], wrecv_sem)
    for k in range(SNODES):
        wait_for(erecv.at[k, pl.ds(0, POLES - 1)], erecv_sem.at[k])
        straight = jnp.zeros((ROWS, LANES), jnp.float32)
        crossed = jnp.zeros((ROWS, LANES), jnp.float32)
        for p in range(POLES):
            value = erecv[k, p].astype(jnp.float32)
            straight = straight + wrows[p, 0:1, :] * value
            crossed = crossed + wrows[p, 1:2, :] * value
        column_out[k] = straight + turned(crossed)

    wait_for(drecv.at[pl.ds(0, RING - 1)], drecv_sem)
    summed = drecv[0]
    for source in range(1, RING):
        summed = summed + drecv[source]
    diag_out[...] = summed

    for k in range(SNODES):
        cross(k).wait_send()
        wait_for(fbuf.at[k, pl.ds(0, 62)], ag_sent.at[k])
        wait_for(esend.at[k, pl.ds(0, POLES - 1)], esent.at[k])
        wait_for(tsend.at[k, pl.ds(0, IN_PLANE - 1)], tsent.at[k])
    wait_for(dsend.at[pl.ds(0, RING - 1)], dsent)
    wait_for(wrows.at[pl.ds(0, POLES - 1)], wsent)


def body(inverse_rows, factor, diag_inverse, pole_weights, structure, row_owner):
    rows = inverse_rows.reshape(2 * ROWS, inverse_rows.shape[3])
    by_pole = factor.reshape(SNODES, SHARD, 2, POLES, 64).transpose(0, 1, 3, 2, 4)
    by_pole = by_pole.reshape(SNODES, SHARD, 2 * BLOCK)
    diag = diag_inverse.reshape(SNODES, POLES, 64, 2, 8).transpose(0, 4, 1, 3, 2)
    diag = diag.reshape(SNODES, 8, 2 * BLOCK)
    smem = pl.BlockSpec(memory_space=pltpu.SMEM)
    vmem = pl.BlockSpec(memory_space=pltpu.VMEM)
    dma = pltpu.SemaphoreType.DMA
    column, diagonal = pl.pallas_call(
        kernel,
        out_shape=(
            jax.ShapeDtypeStruct((SNODES, ROWS, LANES), jnp.float32),
            jax.ShapeDtypeStruct((SNODES, 8, LANES), jnp.float32),
        ),
        in_specs=[smem, smem, smem, vmem, pl.BlockSpec(memory_space=pl.ANY), vmem],
        out_specs=(vmem, vmem),
        scratch_shapes=[
            pltpu.VMEM((SNODES, 64, SHARD, 2 * BLOCK), jnp.bfloat16),
            pltpu.VMEM((2 * ROWS, 8192), jnp.bfloat16),
            pltpu.VMEM((SNODES, POLES, ROWS, LANES), jnp.bfloat16),
            pltpu.VMEM((SNODES, POLES, ROWS, LANES), jnp.bfloat16),
            pltpu.VMEM((SNODES, IN_PLANE, SHARD, LANES), jnp.bfloat16),
            pltpu.VMEM((SNODES, IN_PLANE, SHARD, LANES), jnp.bfloat16),
            pltpu.VMEM((RING, SNODES, 8, LANES), jnp.float32),
            pltpu.VMEM((RING, SNODES, 8, LANES), jnp.float32),
            pltpu.VMEM((POLES, 8, LANES), jnp.float32),
            dma,
            dma((4, 20)),
            dma((SNODES,)),
            dma((SNODES,)),
            dma((SNODES,)),
            dma((SNODES,)),
            dma,
            dma,
            dma((SNODES,)),
            dma((SNODES,)),
            dma((SNODES,)),
            dma((SNODES,)),
            dma,
            dma,
        ],
        compiler_params=pltpu.CompilerParams(
            collective_id=0, has_side_effects=True, vmem_limit_bytes=48 * 1024 * 1024
        ),
    )(structure, row_owner, pole_weights, by_pole, rows, diag)
    column_sum = column.reshape(SNODES, ROWS, 2, 64)
    diagonal_sum = diagonal.reshape(SNODES, 8, 2, 64).transpose(0, 3, 2, 1)
    return (column_sum, diagonal_sum)


def solution(mesh):
    in_specs = (
        P("pole", None, "grid", None),
        P("pole", None, "grid", None, None),
        P("pole", None, None, None, "grid"),
        P("pole", None),
        P(),
        P(),
    )
    out_specs = (P(None, "grid", None, "pole"), P(None, "pole", None, "grid"))
    return jax.shard_map(body, mesh=mesh, in_specs=in_specs, out_specs=out_specs, check_vma=False)
```

time: 310 us -> 95.1 us (0.31)
  waiting for transfers between devices: 181 us -> 0 us
  Pallas kernels: 0 us -> 85.9 us
  starting transfers between devices: 43.8 us -> 0 us
  between operations: 41 us -> 0.68 us
  local copies, waits for them, and re-layouts: 28.8 us -> 8.35 us
  other arithmetic: 7.44 us -> 0 us
  matrix products: 6.24 us -> 0 us
    all_gather x1 -> x0, waiting for transfers between devices: 147 us -> none  [side_by_side(): lax.all_gather(both, axis, axis=dim, tiled=True)]
    pallas_call x0 -> x1, Pallas kernels: none -> 85.9 us  [body(): pl.pallas_call(kernel, out_shape=(jax.ShapeDtypeStruct((SNODES, ROWS, LAN...]
    all_to_all x4 -> x0, starting transfers between devices: 43.8 us -> none  [the longest x1 13.1 us: copy_for_each(): lax.all_to_all(jnp.broadcast_to(array[None], (devices, *array.shape)), ax...]
    all_to_all x4 -> x0, waiting for transfers between devices: 33.7 us -> none  [the longest x1 14.2 us: body(): lax.all_to_all(outgoing, 'pole', split_axis=3, concat_axis=3, tiled=True)]
    split x1 -> x0, local copies, waits for them, and re-layouts: 10.8 us -> none  [side_by_side(): jnp.split(lax.all_gather(both, axis, axis=dim, tiled=True), ends, axis=al...]
    dot_general x4 -> x0, matrix products: 6.24 us -> none  [the longest x2 3.65 us: body(): lax.dot_general(factors[snode_id].reshape(span_rows, 2 * BLOCK), right_pa...]
    unnamed x17 -> x8, local copies, waits for them, and re-layouts: 7.67 us -> 4.17 us
    reshape x0 -> x8, local copies, waits for them, and re-layouts: none -> 3.42 us  [the longest x2 1.34 us: body(): factor.reshape(SNODES, SHARD, 2, POLES, 64).transpose(0, 1, 3, 2, 4)]
  transfers between devices with their start and end apart: 5 -> 0, of which waited for: 4 -> 0; matrix products, arithmetic and copies ran while one was open for 12% -> 0% of each run, Pallas kernels for 0% -> 0%
where the time goes in v1:
time: 95.1 us; the launch traced here: 94.9 us
  Pallas kernels  85.9 us (90%)
  local copies, waits for them, and re-layouts  8.35 us (9%)
    pallas_call x1, Pallas kernels, body(): pl.pallas_call(kernel, out_shape=(jax.ShapeDtypeStruct((SNODES, ROWS, LAN...  85.9 us
    unnamed x8, local copies, waits for them, and re-layouts  4.17 us

profile of v1, /device:TPU:1, one launch (start us, length us, event | category | flops | bytes accessed | tf_op | source)
XLA Modules:
  0.0 94.9 jit_solution(4958555589034439559)
XLA Ops:
  0.6 1.1 %reshape.25 = bf16[2,32,2,8,64]{4,3,2,1,0:T(8,128)(2,1)S(1)} reshape(bf16[1,2,32,2,512]{4,3,2,1,0:T(2,128)(2,1)} %param.7) | data formatting | bytes 262144 | tf_op jit(solution)/shard_map/reshape | solution.py:328
  1.8 0.2 copy.19
  2.0 0.2 reshape.26.factor
  2.2 0.9 reshape.28
  3.1 0.1 copy.20
  3.2 0.2 reshape.29.diag
  3.4 0.0 copy-start
  3.4 2.2 %copy-done = bf16[1,2,128,8192]{3,2,1,0:T(8,128)(2,1)S(1)} copy-done((bf16[1,2,128,8192]{3,2,1,0:T(8,128)(2,1)S(1)}, bf16[1,2,128,8192]{3,2,1,0:T(8,128)(2,1)}, u32[]{:S(2)}) %copy-start) | copy-done | bytes 4194328
  5.6 0.0 copy-start.1
  5.6 0.7 copy-done.1
  6.3 0.0 copy-start.2
  6.3 0.7 copy-done.2
  6.9 0.0 copy-start.3
  6.9 0.7 copy-done.3
  7.6 85.9 %shard_map.77 = (f32[2,128,128]{2,1,0:T(8,128)S(1)}, f32[2,8,128]{2,1,0:T(8,128)S(1)}) custom-call(s32[2,4]{1,0:T(2,128)S(1)} %copy-done.1, s32[16]{0:T(128)S(1)} %copy-done.2, f32[1,2]{1,0:T(1,128)S(1)} %copy-done.3, bf16[2,32,1024]{2,1,0:T(8,128)(2,1)S(1)} %reshape.26.factor, bf16[256,8192]{1,0:T(8,128)(2,1)S(1)} %bitcast.15, f32[2,8,1024]{2,1,0:T(8,128)S(1)} %reshape.29.diag), custom_call_target="tpu_custom_call" | custom-call | tf_op jit(solution)/shard_map/pallas_call | solution.py:335
  93.5 0.8 copy.14
  94.2 0.1 reshape.31
  94.3 0.6 copy.21
Async XLA Ops:
  3.4 2.2 %copy-start = (bf16[1,2,128,8192]{3,2,1,0:T(8,128)(2,1)S(1)}, bf16[1,2,128,8192]{3,2,1,0:T(8,128)(2,1)}, u32[]{:S(2)}) copy-start(bf16[1,2,128,8192]{3,2,1,0:T(8,128)(2,1)} %param.6) | copy-start | bytes 12582916
  5.6 0.7 copy-start.1
  6.3 0.7 copy-start.2
  6.9 0.7 copy-start.3

commit v2 on v1

--- a/solution.py
+++ b/solution.py
@@ -20,16 +20,16 @@
 DOT = (((1,), (0,)), ((), ()))
 
 ORDER = (
-    (0, 0), (1, 0), (0, 2), (2, 0), (1, 2), (3, 0), (2, 2), (0, 1), (4, 0), (3, 2), (1, 1), (4, 2),
-    (0, 3), (2, 1), (1, 3), (3, 1), (2, 3), (4, 1), "first", (3, 3), (4, 3), "second",
+    (0, 0), (0, 2), (1, 0), (1, 2), (2, 0), (2, 2), (3, 0), (0, 1), (3, 2), (4, 0), (1, 1), (4, 2),
+    (0, 3), (2, 1), (1, 3), (3, 1), (2, 3), (4, 1), (3, 3), "first", (4, 3), "second", "moments",
 )
 ROUNDS = ((0, 0), (0, 1), (1, 0), (1, 1))
 
 
 def kernel(
-    structure, row_owner, weights, factor, rows_hbm, diag,
+    structure_hbm, row_owner_hbm, weights_hbm, factor, rows_hbm, diag,
     column_out, diag_out,
-    fbuf, rows, esend, erecv, tsend, trecv, dsend, drecv, wrows,
+    structure, row_owner, weights, small_sem, fbuf, rows, esend, erecv, tsend, trecv, dsend, drecv, wrows,
     rows_sem, ag_sem, cross_sem, pair_sem, erecv_sem, trecv_sem, drecv_sem, wrecv_sem,
     ag_sent, cross_sent, esent, tsent, dsent, wsent,
 ):
@@ -56,9 +56,14 @@
 
     load_rows = pltpu.make_async_copy(rows_hbm, rows, rows_sem)
     load_rows.start()
-
-    part = lax.broadcasted_iota(jnp.int32, (8, LANES), 0)
-    wrows[pole] = jnp.where(part == 0, weights[0, 0], weights[0, 1])
+    small = [
+        pltpu.make_async_copy(source, target, small_sem.at[i])
+        for i, (source, target) in enumerate(
+            ((structure_hbm, structure), (row_owner_hbm, row_owner), (weights_hbm, weights))
+        )
+    ]
+    for load in small:
+        load.start()
 
     barrier = pltpu.get_barrier_semaphore()
 
@@ -76,6 +81,10 @@
     lax.fori_loop(1, RING, greet_height, 0)
     for k in range(SNODES):
         fbuf[k, grid] = factor[k]
+    for load in small:
+        load.wait()
+    part = lax.broadcasted_iota(jnp.int32, (8, LANES), 0)
+    wrows[pole] = jnp.where(part == 0, weights[0, 0], weights[0, 1])
     pl.semaphore_wait(barrier, IN_PLANE - 1 + RING - 1)
 
     def copy(src, dst, sent, received, device):
@@ -198,13 +207,18 @@
         for i in range(LISTED):
             active = active + jnp.where(owners[k][i] == grid // 4, 1, 0)
         active = active.astype(jnp.float32)
-        for n in range(4):
+
+        def chunk(step, carry):
+            n = (x + 1 + step) % SIDE
+            start = pl.multiple_of(2 * LANES * n, 2 * LANES)
             product = jnp.zeros((2 * ROWS, 2 * LANES), jnp.float32)
             for i in range(LISTED):
-                start = structure[k, i] * BLOCK
-                block = fbuf[k, pl.ds(16 * i, 16), :, pl.ds(256 * n, 256)].reshape(BLOCK, 256)
+                block = fbuf[k, pl.ds(16 * i, 16), :, pl.ds(start, 2 * LANES)]
                 product = product + lax.dot_general(
-                    rows[:, pl.ds(start, BLOCK)], block, DOT, preferred_element_type=jnp.float32
+                    rows[:, pl.ds(structure[k, i] * BLOCK, BLOCK)],
+                    block.reshape(BLOCK, 2 * LANES),
+                    DOT,
+                    preferred_element_type=jnp.float32,
                 )
             flipped = []
             for u in range(2):
@@ -221,24 +235,32 @@
                 ]
                 tsend[k, 8 * n + h] = jnp.concatenate(pieces, axis=0).astype(jnp.bfloat16)
 
-        def send_column(step, carry):
-            target = (pole + step) % POLES
-            copy(
-                esend.at[k, target], erecv.at[k, pole], esent.at[k], erecv_sem.at[k],
-                (target, grid),
-            ).start()
+            def send_tile(h, inner):
+                target = 8 * n + (y * 2 + core + 1 + h) % 8
+
+                @pl.when(target != seat)
+                def _():
+                    copy(
+                        tsend.at[k, target], trecv.at[k, seat], tsent.at[k], trecv_sem.at[k],
+                        (pole, seat_grid(target)),
+                    ).start()
+
+                return inner
+
+            lax.fori_loop(0, 8, send_tile, 0)
+            for u in range(2):
+                target = 2 * n + u
+
+                @pl.when(target != pole)
+                def _(target=target):
+                    copy(
+                        esend.at[k, target], erecv.at[k, pole], esent.at[k], erecv_sem.at[k],
+                        (target, grid),
+                    ).start()
+
             return carry
 
-        def send_tile(step, carry):
-            target = (seat + step) % IN_PLANE
-            copy(
-                tsend.at[k, target], trecv.at[k, seat], tsent.at[k], trecv_sem.at[k],
-                (pole, seat_grid(target)),
-            ).start()
-            return carry
-
-        lax.fori_loop(1, IN_PLANE, send_tile, 0)
-        lax.fori_loop(1, POLES, send_column, 0)
+        lax.fori_loop(0, SIDE, chunk, 0)
         erecv[k, pole] = esend[k, pole]
         trecv[k, seat] = tsend[k, seat]
 
@@ -258,10 +280,39 @@
         for j in range(POLES):
             lanes = slice(LANES * j, LANES * (j + 1))
             moment = total[:16, lanes] + turned(total[16:, lanes])
+            at_128 = slice(LANES * (j // 2), LANES * (j // 2 + 1))
+            diag_real, diag_imag = diag[k, 0, :, at_128], diag[k, 1, :, at_128]
+            if j % 2 == 0:
+                given = jnp.where(lane < 64, diag_real, pltpu.roll(diag_imag, 64, 1))
+            else:
+                given = jnp.where(lane < 64, pltpu.roll(diag_real, 64, 1), diag_imag)
             for side in range(2):
                 mine = jnp.where(plane == side, 1.0, 0.0).astype(jnp.float32)
-                value = mine * diag[k, :, lanes] - moment[8 * side : 8 * side + 8]
-                dsend[8 * side + j, k] = weight_real * value + weight_imag * turned(value)
+                value = mine * given - moment[8 * side : 8 * side + 8]
+                dsend[k, 8 * side + j] = weight_real * value + weight_imag * turned(value)
+
+        def send_diag(step, carry):
+            target = (height + step) % RING
+            copy(
+                dsend.at[k, target], drecv.at[k, height], dsent.at[k], drecv_sem.at[k],
+                height_device(target),
+            ).start()
+            return carry
+
+        lax.fori_loop(1, RING, send_diag, 0)
+        drecv[k, height] = dsend[k, height]
+
+    def sum_columns(k):
+        wait_for(erecv.at[k, pl.ds(0, POLES - 1)], erecv_sem.at[k])
+        straight = jnp.zeros((ROWS, LANES), jnp.float32)
+        crossed = jnp.zeros((ROWS, LANES), jnp.float32)
+        for p in range(POLES):
+            value = erecv[k, p].astype(jnp.float32)
+            straight = straight + wrows[p, 0:1, :] * value
+            crossed = crossed + wrows[p, 1:2, :] * value
+        flat = jnp.transpose(straight + turned(crossed))
+        column_out[k, 0] = flat[:64]
+        column_out[k, 1] = flat[64:]
 
     owners = []
     for k in range(SNODES):
@@ -281,45 +332,29 @@
             columns(0)
         elif entry == "second":
             columns(1)
+        elif entry == "moments":
+            moments(0)
         else:
             stage(*entry)
 
+    moments(1)
+    wait_for(wrows.at[pl.ds(0, POLES - 1)], wrecv_sem)
+    sum_columns(0)
+    sum_columns(1)
     for k in range(SNODES):
-        moments(k)
-
-    def send_diag(step, carry):
-        target = (height + step) % RING
-        copy(
-            dsend.at[target], drecv.at[height], dsent, drecv_sem, height_device(target)
-        ).start()
-        return carry
-
-    lax.fori_loop(1, RING, send_diag, 0)
-    drecv[height] = dsend[height]
-
-    wait_for(wrows.at[pl.ds(0, POLES - 1)], wrecv_sem)
-    for k in range(SNODES):
-        wait_for(erecv.at[k, pl.ds(0, POLES - 1)], erecv_sem.at[k])
-        straight = jnp.zeros((ROWS, LANES), jnp.float32)
-        crossed = jnp.zeros((ROWS, LANES), jnp.float32)
-        for p in range(POLES):
-            value = erecv[k, p].astype(jnp.float32)
-            straight = straight + wrows[p, 0:1, :] * value
-            crossed = crossed + wrows[p, 1:2, :] * value
-        column_out[k] = straight + turned(crossed)
-
-    wait_for(drecv.at[pl.ds(0, RING - 1)], drecv_sem)
-    summed = drecv[0]
-    for source in range(1, RING):
-        summed = summed + drecv[source]
-    diag_out[...] = summed
+        wait_for(drecv.at[k, pl.ds(0, RING - 1)], drecv_sem.at[k])
+        summed = drecv[k, 0]
+        for source in range(1, RING):
+            summed = summed + drecv[k, source]
+        diag_out[k, 0] = summed[:, :64]
+        diag_out[k, 1] = pltpu.roll(summed, 64, 1)[:, :64]
 
     for k in range(SNODES):
         cross(k).wait_send()
         wait_for(fbuf.at[k, pl.ds(0, 62)], ag_sent.at[k])
         wait_for(esend.at[k, pl.ds(0, POLES - 1)], esent.at[k])
         wait_for(tsend.at[k, pl.ds(0, IN_PLANE - 1)], tsent.at[k])
-    wait_for(dsend.at[pl.ds(0, RING - 1)], dsent)
+        wait_for(dsend.at[k, pl.ds(0, RING - 1)], dsent.at[k])
     wait_for(wrows.at[pl.ds(0, POLES - 1)], wsent)
 
 
@@ -327,28 +362,31 @@
     rows = inverse_rows.reshape(2 * ROWS, inverse_rows.shape[3])
     by_pole = factor.reshape(SNODES, SHARD, 2, POLES, 64).transpose(0, 1, 3, 2, 4)
     by_pole = by_pole.reshape(SNODES, SHARD, 2 * BLOCK)
-    diag = diag_inverse.reshape(SNODES, POLES, 64, 2, 8).transpose(0, 4, 1, 3, 2)
-    diag = diag.reshape(SNODES, 8, 2 * BLOCK)
-    smem = pl.BlockSpec(memory_space=pltpu.SMEM)
+    diag = diag_inverse[0].transpose(0, 2, 3, 1)
+    hbm = pl.BlockSpec(memory_space=pltpu.HBM)
     vmem = pl.BlockSpec(memory_space=pltpu.VMEM)
     dma = pltpu.SemaphoreType.DMA
     column, diagonal = pl.pallas_call(
         kernel,
         out_shape=(
-            jax.ShapeDtypeStruct((SNODES, ROWS, LANES), jnp.float32),
-            jax.ShapeDtypeStruct((SNODES, 8, LANES), jnp.float32),
+            jax.ShapeDtypeStruct((SNODES, 2, 64, ROWS), jnp.float32),
+            jax.ShapeDtypeStruct((SNODES, 2, 8, 64), jnp.float32),
         ),
-        in_specs=[smem, smem, smem, vmem, pl.BlockSpec(memory_space=pl.ANY), vmem],
+        in_specs=[hbm, hbm, hbm, vmem, hbm, vmem],
         out_specs=(vmem, vmem),
         scratch_shapes=[
+            pltpu.SMEM((SNODES, LISTED), jnp.int32),
+            pltpu.SMEM((16,), jnp.int32),
+            pltpu.SMEM((1, 2), jnp.float32),
+            dma((3,)),
             pltpu.VMEM((SNODES, 64, SHARD, 2 * BLOCK), jnp.bfloat16),
             pltpu.VMEM((2 * ROWS, 8192), jnp.bfloat16),
             pltpu.VMEM((SNODES, POLES, ROWS, LANES), jnp.bfloat16),
             pltpu.VMEM((SNODES, POLES, ROWS, LANES), jnp.bfloat16),
             pltpu.VMEM((SNODES, IN_PLANE, SHARD, LANES), jnp.bfloat16),
             pltpu.VMEM((SNODES, IN_PLANE, SHARD, LANES), jnp.bfloat16),
-            pltpu.VMEM((RING, SNODES, 8, LANES), jnp.float32),
-            pltpu.VMEM((RING, SNODES, 8, LANES), jnp.float32),
+            pltpu.VMEM((SNODES, RING, 8, LANES), jnp.float32),
+            pltpu.VMEM((SNODES, RING, 8, LANES), jnp.float32),
             pltpu.VMEM((POLES, 8, LANES), jnp.float32),
             dma,
             dma((4, 20)),
@@ -356,21 +394,21 @@
             dma((SNODES,)),
             dma((SNODES,)),
             dma((SNODES,)),
+            dma((SNODES,)),
             dma,
-            dma,
-            dma((SNODES,)),
-            dma((SNODES,)),
-            dma((SNODES,)),
-            dma((SNODES,)),
-            dma,
+            dma((SNODES,)),
+            dma((SNODES,)),
+            dma((SNODES,)),
+            dma((SNODES,)),
+            dma((SNODES,)),
             dma,
         ],
         compiler_params=pltpu.CompilerParams(
-            collective_id=0, has_side_effects=True, vmem_limit_bytes=48 * 1024 * 1024
+            collective_id=0, has_side_effects=True, vmem_limit_bytes=60 * 1024 * 1024
         ),
     )(structure, row_owner, pole_weights, by_pole, rows, diag)
-    column_sum = column.reshape(SNODES, ROWS, 2, 64)
-    diagonal_sum = diagonal.reshape(SNODES, 8, 2, 64).transpose(0, 3, 2, 1)
+    column_sum = column.transpose(0, 3, 1, 2)
+    diagonal_sum = diagonal.transpose(0, 3, 1, 2)
     return (column_sum, diagonal_sum)
 
 

time: 95.1 us -> 90.7 us (0.954)
  local copies, waits for them, and re-layouts: 8.35 us -> 5.09 us
  Pallas kernels: 85.9 us -> 84.7 us
    reshape x5 -> x0, local copies, waits for them, and re-layouts: 1.89 us -> none  [the longest x2 1.03 us: body(): diag_inverse.reshape(SNODES, POLES, 64, 2, 8).transpose(0, 4, 1, 3, 2)]
    unnamed x8 -> x2, local copies, waits for them, and re-layouts: 4.17 us -> 2.89 us
    pallas_call x1, Pallas kernels: 85.9 us -> 84.7 us  [body(): pl.pallas_call(kernel, out_shape=(jax.ShapeDtypeStruct((SNODES, 2, 64, RO...]
where the time goes in v2:
time: 90.7 us; the launch traced here: 90.5 us
  Pallas kernels  84.7 us (93%)
  local copies, waits for them, and re-layouts  5.09 us (6%)
    pallas_call x1, Pallas kernels, body(): pl.pallas_call(kernel, out_shape=(jax.ShapeDtypeStruct((SNODES, 2, 64, RO...  84.7 us
    unnamed x2, local copies, waits for them, and re-layouts  2.89 us

profile of v2, /device:TPU:1, one launch (start us, length us, event | category | flops | bytes accessed | tf_op | source)
XLA Modules:
  0.0 90.5 jit_solution(16719911728981498172)
XLA Ops:
  0.6 1.1 %reshape.13 = bf16[2,32,2,8,64]{4,3,2,1,0:T(8,128)(2,1)S(1)} reshape(bf16[1,2,32,2,512]{4,3,2,1,0:T(2,128)(2,1)} %param.7) | data formatting | bytes 262144 | tf_op jit(solution)/shard_map/reshape | solution.py:363
  1.8 0.2 copy.10
  2.0 0.9 reshape.14.factor
  2.8 84.7 %shard_map.77 = (f32[2,2,64,128]{3,2,1,0:T(8,128)}, f32[2,2,8,64]{3,2,1,0:T(8,128)}) custom-call(s32[2,4]{1,0:T(2,128)} %structure_hbm.1, s32[16]{0:T(128)} %row_owner_hbm.1, f32[1,2]{1,0:T(1,128)} %weights_hbm.1, bf16[2,32,1024]{2,1,0:T(8,128)(2,1)} %reshape.14.factor, bf16[256,8192]{1,0:T(8,128)(2,1)} %bitcast.9, f32[2,2,8,512]{3,2,1,0:T(8,128)} %bitcast.12), custom_call_target="tpu_custom_call" | custom-call | tf_op jit(solution)/shard_map/pallas_call | solution.py:369
  87.6 1.6 %copy.13 = f32[2,128,2,64]{1,3,2,0:T(8,128)} copy(f32[2,128,2,64]{1,3,2,0:T(8,128)} %bitcast.11) | data formatting | bytes 262144
  89.1 1.3 %copy.14 = f32[2,64,2,8]{1,3,2,0:T(8,128)} copy(f32[2,64,2,8]{1,3,2,0:T(8,128)} %bitcast.13) | data formatting | bytes 16384

commit v3 on v2

--- a/solution.py
+++ b/solution.py
@@ -9,6 +9,7 @@
 LISTED = 4
 SNODES = 2
 POLES = 8
+HALF = 4
 PLANES = 2
 SIDE = 4
 IN_PLANE = 32
@@ -29,9 +30,9 @@
 def kernel(
     structure_hbm, row_owner_hbm, weights_hbm, factor, rows_hbm, diag,
     column_out, diag_out,
-    structure, row_owner, weights, small_sem, fbuf, rows, esend, erecv, tsend, trecv, dsend, drecv, wrows,
-    rows_sem, ag_sem, cross_sem, pair_sem, erecv_sem, trecv_sem, drecv_sem, wrecv_sem,
-    ag_sent, cross_sent, esent, tsent, dsent, wsent,
+    structure, row_owner, weights, small_sem, fbuf, rows, esend, erecv, psend, precv, tsend, trecv, dsend, drecv, wrows,
+    rows_sem, ag_sem, cross_sem, pair_sem, erecv_sem, precv_sem, trecv_sem, drecv_sem, wrecv_sem,
+    ag_sent, cross_sent, esent, psent, tsent, dsent, wsent,
 ):
     pole = lax.axis_index("pole")
     grid = lax.axis_index("grid")
@@ -39,6 +40,7 @@
     y, core = (grid // 2) % 4, grid % 2
     seat = x * 8 + y * 2 + core
     height = plane * 8 + pole
+    quad, member = pole // HALF, pole % HALF
 
     def at(x_to, plane_to, y_to, core_to):
         return x_to * 16 + plane_to * 8 + y_to * 2 + core_to
@@ -198,7 +200,7 @@
     def weight_send(step):
         return copy(
             wrows.at[pole], wrows.at[pole], wsent, wrecv_sem,
-            ((pole + step) % POLES, grid),
+            (quad * HALF + (member + step) % HALF, grid),
         )
 
     def columns(k):
@@ -249,19 +251,22 @@
 
             lax.fori_loop(0, 8, send_tile, 0)
             for u in range(2):
-                target = 2 * n + u
-
-                @pl.when(target != pole)
-                def _(target=target):
+                chunk_id = 2 * n + u
+                owner = chunk_id % HALF
+                slot = (chunk_id // HALF) * HALF + member
+
+                @pl.when(owner != member)
+                def _(chunk_id=chunk_id, owner=owner, slot=slot):
                     copy(
-                        esend.at[k, target], erecv.at[k, pole], esent.at[k], erecv_sem.at[k],
-                        (target, grid),
+                        esend.at[k, chunk_id], erecv.at[k, slot], esent.at[k], erecv_sem.at[k],
+                        (quad * HALF + owner, grid),
                     ).start()
 
             return carry
 
         lax.fori_loop(0, SIDE, chunk, 0)
-        erecv[k, pole] = esend[k, pole]
+        for part in range(2):
+            erecv[k, part * HALF + member] = esend[k, part * HALF + member]
         trecv[k, seat] = tsend[k, seat]
 
     def moments(k):
@@ -302,15 +307,30 @@
         lax.fori_loop(1, RING, send_diag, 0)
         drecv[k, height] = dsend[k, height]
 
-    def sum_columns(k):
-        wait_for(erecv.at[k, pl.ds(0, POLES - 1)], erecv_sem.at[k])
+    def partner_send(k):
+        return copy(
+            psend.at[k], precv.at[k], psent.at[k], precv_sem.at[k],
+            ((pole + HALF) % POLES, grid),
+        )
+
+    def half_sum(k, part):
         straight = jnp.zeros((ROWS, LANES), jnp.float32)
         crossed = jnp.zeros((ROWS, LANES), jnp.float32)
-        for p in range(POLES):
-            value = erecv[k, p].astype(jnp.float32)
-            straight = straight + wrows[p, 0:1, :] * value
-            crossed = crossed + wrows[p, 1:2, :] * value
-        flat = jnp.transpose(straight + turned(crossed))
+        for r in range(HALF):
+            value = erecv[k, part * HALF + r].astype(jnp.float32)
+            straight = straight + wrows[quad * HALF + r, 0:1, :] * value
+            crossed = crossed + wrows[quad * HALF + r, 1:2, :] * value
+        return straight + turned(crossed)
+
+    def send_half(k):
+        wait_for(erecv.at[k, pl.ds(0, 2 * HALF - 2)], erecv_sem.at[k])
+        psend[k] = half_sum(k, 1 - quad).astype(jnp.bfloat16)
+        partner_send(k).start()
+
+    def sum_columns(k):
+        own = half_sum(k, quad)
+        partner_send(k).wait_recv()
+        flat = jnp.transpose(own + precv[k].astype(jnp.float32))
         column_out[k, 0] = flat[:64]
         column_out[k, 1] = flat[64:]
 
@@ -323,7 +343,7 @@
                 owner = owner + jnp.where(structure[k, i] == ancestor, row_owner[ancestor], 0)
             owners[k].append(owner)
 
-    for step in range(1, POLES):
+    for step in range(1, HALF):
         weight_send(step).start()
 
     for entry in ORDER:
@@ -337,8 +357,10 @@
         else:
             stage(*entry)
 
+    wait_for(wrows.at[pl.ds(0, HALF - 1)], wrecv_sem)
+    send_half(0)
     moments(1)
-    wait_for(wrows.at[pl.ds(0, POLES - 1)], wrecv_sem)
+    send_half(1)
     sum_columns(0)
     sum_columns(1)
     for k in range(SNODES):
@@ -352,10 +374,11 @@
     for k in range(SNODES):
         cross(k).wait_send()
         wait_for(fbuf.at[k, pl.ds(0, 62)], ag_sent.at[k])
-        wait_for(esend.at[k, pl.ds(0, POLES - 1)], esent.at[k])
+        wait_for(esend.at[k, pl.ds(0, 2 * HALF - 2)], esent.at[k])
+        partner_send(k).wait_send()
         wait_for(tsend.at[k, pl.ds(0, IN_PLANE - 1)], tsent.at[k])
         wait_for(dsend.at[k, pl.ds(0, RING - 1)], dsent.at[k])
-    wait_for(wrows.at[pl.ds(0, POLES - 1)], wsent)
+    wait_for(wrows.at[pl.ds(0, HALF - 1)], wsent)
 
 
 def body(inverse_rows, factor, diag_inverse, pole_weights, structure, row_owner):
@@ -383,6 +406,8 @@
             pltpu.VMEM((2 * ROWS, 8192), jnp.bfloat16),
             pltpu.VMEM((SNODES, POLES, ROWS, LANES), jnp.bfloat16),
             pltpu.VMEM((SNODES, POLES, ROWS, LANES), jnp.bfloat16),
+            pltpu.VMEM((SNODES, ROWS, LANES), jnp.bfloat16),
+            pltpu.VMEM((SNODES, ROWS, LANES), jnp.bfloat16),
             pltpu.VMEM((SNODES, IN_PLANE, SHARD, LANES), jnp.bfloat16),
             pltpu.VMEM((SNODES, IN_PLANE, SHARD, LANES), jnp.bfloat16),
             pltpu.VMEM((SNODES, RING, 8, LANES), jnp.float32),
@@ -395,7 +420,9 @@
             dma((SNODES,)),
             dma((SNODES,)),
             dma((SNODES,)),
+            dma((SNODES,)),
             dma,
+            dma((SNODES,)),
             dma((SNODES,)),
             dma((SNODES,)),
             dma((SNODES,)),

time: 90.7 us -> 82.9 us (0.914)
  Pallas kernels: 84.7 us -> 76.2 us
    pallas_call x1, Pallas kernels: 84.7 us -> 76.2 us  [body(): pl.pallas_call(kernel, out_shape=(jax.ShapeDtypeStruct((SNODES, 2, 64, RO...]
where the time goes in v3:
time: 82.9 us; the launch traced here: 81.9 us
  Pallas kernels  76.2 us (92%)
  local copies, waits for them, and re-layouts  5.09 us (6%)
    pallas_call x1, Pallas kernels, body(): pl.pallas_call(kernel, out_shape=(jax.ShapeDtypeStruct((SNODES, 2, 64, RO...  76.2 us
    unnamed x2, local copies, waits for them, and re-layouts  2.89 us

profile of v3, /device:TPU:1, one launch (start us, length us, event | category | flops | bytes accessed | tf_op | source)
XLA Modules:
  0.0 81.9 jit_solution(2084553684738188988)
XLA Ops:
  0.6 1.1 %reshape.13 = bf16[2,32,2,8,64]{4,3,2,1,0:T(8,128)(2,1)S(1)} reshape(bf16[1,2,32,2,512]{4,3,2,1,0:T(2,128)(2,1)} %param.7) | data formatting | bytes 262144 | tf_op jit(solution)/shard_map/reshape | solution.py:386
  1.8 0.2 copy.10
  2.0 0.9 %reshape.14.factor = bf16[2,32,1024]{2,1,0:T(8,128)(2,1)} reshape(bf16[2,32,8,2,64]{4,3,2,1,0:T(2,128)(2,1)S(1)} %bitcast.10) | data formatting | bytes 262144 | tf_op jit(solution)/shard_map/reshape | solution.py:387
  2.8 76.2 %shard_map.77 = (f32[2,2,64,128]{3,2,1,0:T(8,128)}, f32[2,2,8,64]{3,2,1,0:T(8,128)}) custom-call(s32[2,4]{1,0:T(2,128)} %structure_hbm.1, s32[16]{0:T(128)} %row_owner_hbm.1, f32[1,2]{1,0:T(1,128)} %weights_hbm.1, bf16[2,32,1024]{2,1,0:T(8,128)(2,1)} %reshape.14.factor, bf16[256,8192]{1,0:T(8,128)(2,1)} %bitcast.9, f32[2,2,8,512]{3,2,1,0:T(8,128)} %bitcast.12), custom_call_target="tpu_custom_call" | custom-call | tf_op jit(solution)/shard_map/pallas_call | solution.py:392
  79.0 1.6 %copy.13 = f32[2,128,2,64]{1,3,2,0:T(8,128)} copy(f32[2,128,2,64]{1,3,2,0:T(8,128)} %bitcast.11) | data formatting | bytes 262144
  80.6 1.3 %copy.14 = f32[2,64,2,8]{1,3,2,0:T(8,128)} copy(f32[2,64,2,8]{1,3,2,0:T(8,128)} %bitcast.13) | data formatting | bytes 16384

commit v4 on v3

--- a/solution.py
+++ b/solution.py
@@ -294,7 +294,8 @@
             for side in range(2):
                 mine = jnp.where(plane == side, 1.0, 0.0).astype(jnp.float32)
                 value = mine * given - moment[8 * side : 8 * side + 8]
-                dsend[k, 8 * side + j] = weight_real * value + weight_imag * turned(value)
+                weighted = weight_real * value + weight_imag * turned(value)
+                dsend[k, 8 * side + j] = weighted.astype(jnp.bfloat16)
 
         def send_diag(step, carry):
             target = (height + step) % RING
@@ -365,9 +366,9 @@
     sum_columns(1)
     for k in range(SNODES):
         wait_for(drecv.at[k, pl.ds(0, RING - 1)], drecv_sem.at[k])
-        summed = drecv[k, 0]
+        summed = drecv[k, 0].astype(jnp.float32)
         for source in range(1, RING):
-            summed = summed + drecv[k, source]
+            summed = summed + drecv[k, source].astype(jnp.float32)
         diag_out[k, 0] = summed[:, :64]
         diag_out[k, 1] = pltpu.roll(summed, 64, 1)[:, :64]
 
@@ -392,8 +393,8 @@
     column, diagonal = pl.pallas_call(
         kernel,
         out_shape=(
-            jax.ShapeDtypeStruct((SNODES, 2, 64, ROWS), jnp.float32),
-            jax.ShapeDtypeStruct((SNODES, 2, 8, 64), jnp.float32),
+            pltpu.VMEM((SNODES, 2, 64, ROWS), jnp.float32),
+            pltpu.VMEM((SNODES, 2, 8, 64), jnp.float32),
         ),
         in_specs=[hbm, hbm, hbm, vmem, hbm, vmem],
         out_specs=(vmem, vmem),
@@ -410,8 +411,8 @@
             pltpu.VMEM((SNODES, ROWS, LANES), jnp.bfloat16),
             pltpu.VMEM((SNODES, IN_PLANE, SHARD, LANES), jnp.bfloat16),
             pltpu.VMEM((SNODES, IN_PLANE, SHARD, LANES), jnp.bfloat16),
-            pltpu.VMEM((SNODES, RING, 8, LANES), jnp.float32),
-            pltpu.VMEM((SNODES, RING, 8, LANES), jnp.float32),
+            pltpu.VMEM((SNODES, RING, 8, LANES), jnp.bfloat16),
+            pltpu.VMEM((SNODES, RING, 8, LANES), jnp.bfloat16),
             pltpu.VMEM((POLES, 8, LANES), jnp.float32),
             dma,
             dma((4, 20)),

time: 82.9 us -> 77.9 us (0.940); the launches traced: 81.9 us -> 77.8 us
  Pallas kernels: 76.2 us -> 73.7 us
  local copies, waits for them, and re-layouts: 5.09 us -> 3.46 us
    pallas_call x1, Pallas kernels: 76.2 us -> 73.7 us  [body(): pl.pallas_call(kernel, out_shape=(pltpu.VMEM((SNODES, 2, 64, ROWS), jnp.f...]
    unnamed x2, local copies, waits for them, and re-layouts: 2.89 us -> 1.26 us
where the time goes in v4:
time: 77.9 us; the launch traced here: 77.8 us
  Pallas kernels  73.7 us (95%)
  local copies, waits for them, and re-layouts  3.46 us (4%)
    pallas_call x1, Pallas kernels, body(): pl.pallas_call(kernel, out_shape=(pltpu.VMEM((SNODES, 2, 64, ROWS), jnp.f...  73.7 us

profile of v4, /device:TPU:1, one launch (start us, length us, event | category | flops | bytes accessed | tf_op | source)
XLA Modules:
  0.0 77.8 jit_solution(13527596271156313788)
XLA Ops:
  0.6 1.1 %reshape.13 = bf16[2,32,2,8,64]{4,3,2,1,0:T(8,128)(2,1)S(1)} reshape(bf16[1,2,32,2,512]{4,3,2,1,0:T(2,128)(2,1)} %param.7) | data formatting | bytes 262144 | tf_op jit(solution)/shard_map/reshape | solution.py:387
  1.8 0.2 copy.10
  2.0 0.9 %reshape.14.factor = bf16[2,32,1024]{2,1,0:T(8,128)(2,1)} reshape(bf16[2,32,8,2,64]{4,3,2,1,0:T(2,128)(2,1)S(1)} %bitcast.12) | data formatting | bytes 262144 | tf_op jit(solution)/shard_map/reshape | solution.py:388
  2.8 73.7 %shard_map.77 = (f32[2,2,64,128]{3,2,1,0:T(8,128)S(1)}, f32[2,2,8,64]{3,2,1,0:T(8,128)S(1)}) custom-call(s32[2,4]{1,0:T(2,128)} %structure_hbm.1, s32[16]{0:T(128)} %row_owner_hbm.1, f32[1,2]{1,0:T(1,128)} %weights_hbm.1, bf16[2,32,1024]{2,1,0:T(8,128)(2,1)} %reshape.14.factor, bf16[256,8192]{1,0:T(8,128)(2,1)} %bitcast.11, f32[2,2,8,512]{3,2,1,0:T(8,128)} %bitcast.13), custom_call_target="tpu_custom_call" | custom-call | tf_op jit(solution)/shard_map/pallas_call | solution.py:393
  76.5 0.7 copy.13
  77.2 0.6 copy.14

commit v5 on v4

--- a/solution.py
+++ b/solution.py
@@ -69,17 +69,15 @@
 
     barrier = pltpu.get_barrier_semaphore()
 
-    def greet_seat(step, carry):
-        target = seat_grid((seat + step) % IN_PLANE)
-        pl.semaphore_signal(barrier, inc=1, device_id=(pole, target), device_id_type=MESH)
-        return carry
+    beside = [along(1, 0), along(-1, 0), along(0, 1), along(0, -1), at(x, plane, y, 1 - core)]
 
     def greet_height(step, carry):
         target = height_device((height + step) % RING)
         pl.semaphore_signal(barrier, inc=1, device_id=target, device_id_type=MESH)
         return carry
 
-    lax.fori_loop(1, IN_PLANE, greet_seat, 0)
+    for target in beside:
+        pl.semaphore_signal(barrier, inc=1, device_id=(pole, target), device_id_type=MESH)
     lax.fori_loop(1, RING, greet_height, 0)
     for k in range(SNODES):
         fbuf[k, grid] = factor[k]
@@ -87,7 +85,7 @@
         load.wait()
     part = lax.broadcasted_iota(jnp.int32, (8, LANES), 0)
     wrows[pole] = jnp.where(part == 0, weights[0, 0], weights[0, 1])
-    pl.semaphore_wait(barrier, IN_PLANE - 1 + RING - 1)
+    pl.semaphore_wait(barrier, len(beside) + RING - 1)
 
     def copy(src, dst, sent, received, device):
         return pltpu.make_async_remote_copy(

time: 77.9 us -> 77.1 us (0.990)
  Pallas kernels: 73.7 us -> 72.9 us
    pallas_call x1, Pallas kernels: 73.7 us -> 72.9 us  [body(): pl.pallas_call(kernel, out_shape=(pltpu.VMEM((SNODES, 2, 64, ROWS), jnp.f...]
where the time goes in v5:
time: 77.1 us; the launch traced here: 77 us
  Pallas kernels  72.9 us (95%)
  local copies, waits for them, and re-layouts  3.46 us (4%)
    pallas_call x1, Pallas kernels, body(): pl.pallas_call(kernel, out_shape=(pltpu.VMEM((SNODES, 2, 64, ROWS), jnp.f...  72.9 us

profile of v5, /device:TPU:1, one launch (start us, length us, event | category | flops | bytes accessed | tf_op | source)
XLA Modules:
  0.0 77.0 jit_solution(1937407490072108855)
XLA Ops:
  0.6 1.1 %reshape.13 = bf16[2,32,2,8,64]{4,3,2,1,0:T(8,128)(2,1)S(1)} reshape(bf16[1,2,32,2,512]{4,3,2,1,0:T(2,128)(2,1)} %param.7) | data formatting | bytes 262144 | tf_op jit(solution)/shard_map/reshape | solution.py:385
  1.8 0.2 copy.10
  2.0 0.9 %reshape.14.factor = bf16[2,32,1024]{2,1,0:T(8,128)(2,1)} reshape(bf16[2,32,8,2,64]{4,3,2,1,0:T(2,128)(2,1)S(1)} %bitcast.12) | data formatting | bytes 262144 | tf_op jit(solution)/shard_map/reshape | solution.py:386
  2.8 72.9 %shard_map.77 = (f32[2,2,64,128]{3,2,1,0:T(8,128)S(1)}, f32[2,2,8,64]{3,2,1,0:T(8,128)S(1)}) custom-call(s32[2,4]{1,0:T(2,128)} %structure_hbm.1, s32[16]{0:T(128)} %row_owner_hbm.1, f32[1,2]{1,0:T(1,128)} %weights_hbm.1, bf16[2,32,1024]{2,1,0:T(8,128)(2,1)} %reshape.14.factor, bf16[256,8192]{1,0:T(8,128)(2,1)} %bitcast.11, f32[2,2,8,512]{3,2,1,0:T(8,128)} %bitcast.13), custom_call_target="tpu_custom_call" | custom-call | tf_op jit(solution)/shard_map/pallas_call | solution.py:391
  75.7 0.7 copy.13
  76.4 0.6 copy.14

commit v6 on v5

--- a/solution.py
+++ b/solution.py
@@ -21,7 +21,7 @@
 DOT = (((1,), (0,)), ((), ()))
 
 ORDER = (
-    (0, 0), (0, 2), (1, 0), (1, 2), (2, 0), (2, 2), (3, 0), (0, 1), (3, 2), (4, 0), (1, 1), (4, 2),
+    (0, 0), (0, 2), (1, 0), (1, 2), (2, 0), (2, 2), (0, 1), (3, 0), (3, 2), (1, 1), (4, 0), (4, 2),
     (0, 3), (2, 1), (1, 3), (3, 1), (2, 3), (4, 1), (3, 3), "first", (4, 3), "second", "moments",
 )
 ROUNDS = ((0, 0), (0, 1), (1, 0), (1, 1))
@@ -76,9 +76,10 @@
         pl.semaphore_signal(barrier, inc=1, device_id=target, device_id_type=MESH)
         return carry
 
+    lax.fori_loop(8, RING, greet_height, 0)
+    lax.fori_loop(1, 8, greet_height, 0)
     for target in beside:
         pl.semaphore_signal(barrier, inc=1, device_id=(pole, target), device_id_type=MESH)
-    lax.fori_loop(1, RING, greet_height, 0)
     for k in range(SNODES):
         fbuf[k, grid] = factor[k]
     for load in small:

time: 77.1 us -> 76.9 us (level)
  no operation moved by 1% of the time
where the time goes in v6:
time: 76.9 us; the launch traced here: 76.7 us
  Pallas kernels  72.6 us (94%)
  local copies, waits for them, and re-layouts  3.46 us (4%)
    pallas_call x1, Pallas kernels, body(): pl.pallas_call(kernel, out_shape=(pltpu.VMEM((SNODES, 2, 64, ROWS), jnp.f...  72.6 us

profile of v6, /device:TPU:1, one launch (start us, length us, event | category | flops | bytes accessed | tf_op | source)
XLA Modules:
  0.0 76.7 jit_solution(16280570587456322934)
XLA Ops:
  0.6 1.1 %reshape.13 = bf16[2,32,2,8,64]{4,3,2,1,0:T(8,128)(2,1)S(1)} reshape(bf16[1,2,32,2,512]{4,3,2,1,0:T(2,128)(2,1)} %param.7) | data formatting | bytes 262144 | tf_op jit(solution)/shard_map/reshape | solution.py:386
  1.8 0.2 copy.10
  2.0 0.9 %reshape.14.factor = bf16[2,32,1024]{2,1,0:T(8,128)(2,1)} reshape(bf16[2,32,8,2,64]{4,3,2,1,0:T(2,128)(2,1)S(1)} %bitcast.12) | data formatting | bytes 262144 | tf_op jit(solution)/shard_map/reshape | solution.py:387
  2.8 72.6 %shard_map.77 = (f32[2,2,64,128]{3,2,1,0:T(8,128)S(1)}, f32[2,2,8,64]{3,2,1,0:T(8,128)S(1)}) custom-call(s32[2,4]{1,0:T(2,128)} %structure_hbm.1, s32[16]{0:T(128)} %row_owner_hbm.1, f32[1,2]{1,0:T(1,128)} %weights_hbm.1, bf16[2,32,1024]{2,1,0:T(8,128)(2,1)} %reshape.14.factor, bf16[256,8192]{1,0:T(8,128)(2,1)} %bitcast.11, f32[2,2,8,512]{3,2,1,0:T(8,128)} %bitcast.13), custom_call_target="tpu_custom_call" | custom-call | tf_op jit(solution)/shard_map/pallas_call | solution.py:392
  75.5 0.7 copy.13
  76.1 0.6 copy.14
